TPU v7x, 128 devices: a whole 4x4x4 slice. The times are simulated.
128 devices in a mesh: lat: 8 (over y_hi, x), lon: 16 (over z, y_lo, core).
Axes of the slice: x: 4, y: 4 (y_hi: 2, y_lo: 2; y = y_hi * 2 + y_lo), z: 4, core: 2. Of those that a mesh axis runs over, the one named last changes fastest.
Arguments:
- state: float32 [8, 60, 64, 2048], P(None, None, 'lat', 'lon'), may hold values from -6 to 6
- surface: bfloat16 [76, 64, 2048], P(None, 'lat', 'lon'), may hold values from -6 to 6
- layer_one: bfloat16 [556, 768], replicated, may hold values from -0.25 to 0.25
- layer_two: bfloat16 [768, 640], replicated, may hold values from -0.21875 to 0.21875
- layer_three: bfloat16 [640, 512], replicated, may hold values from -0.25 to 0.25
- layer_four: bfloat16 [512, 640], replicated, may hold values from -0.25 to 0.25
- layer_five: bfloat16 [640, 368], replicated, may hold values from -0.25 to 0.25
- lit_columns: int32 [8, 16, 1024], P('lat', 'lon'), may hold values from 0 to 1024, as said below
- row_offset: int32 [64], P('lat'), may hold values from 0 to 383
Outputs:
- new_state: float32 [8, 60, 64, 2048], P(None, None, 'lat', 'lon')
- surface_flux: bfloat16 [8, 64, 2048], P(None, 'lat', 'lon')
Inputs may be any that keep to these rules, and one draw needn't show every extreme that they name: `lit_columns`: in each tile's list the first entries are distinct column numbers in rising order and the rest equal 1024. A tile and the tile 16/2 further along the longitude cycle, in the same latitude tile, list 1024 columns together at most, and some such pair lists exactly 1024 in every draw.
All inputs are finite; a program needn't handle non-finite values.
Results may differ from a plain program's by a relative error of at most 0.015.
Values may be sent and summed in bfloat16 or wider, within the bound.
A program may use at most 64 MiB of HBM per device.

v0:
```python
import jax
import jax.numpy as jnp
from jax import lax
from jax.experimental import pallas as pl
from jax.experimental.pallas import tpu as pltpu
from jax.sharding import PartitionSpec as P

MESH = pl.DeviceIdType.MESH
F32, BF16 = jnp.float32, jnp.bfloat16

N_LAT, N_LON = 8, 16
LEV = 60
ROWS, COLS = 8, 128
FIELD = LEV * ROWS
COURANT = 0.6
STEP = 0.5
SLOPE = 0.15
DYN = 192
NIN, NOUT = 556, 368
H1, H2, H3, H4 = 768, 640, 512, 640

LC = 20
NCH = LEV // LC
HC = LC // 2
PER = 10
GROUPS = LEV // PER
CH = 2
NB = ROWS // CH
OZ = NB

EDGES = ((0, -1), (0, 1), (-1, -1), (-1, 1), (1, -1), (1, 1))


def nt(a, b):
    return lax.dot_general(a, b, (((1,), (1,)), ((), ())), preferred_element_type=F32)


def eye(n):
    return (lax.broadcasted_iota(jnp.int32, (n, n), 0) == lax.broadcasted_iota(jnp.int32, (n, n), 1)).astype(F32).astype(BF16)


def leaky(z):
    return jnp.maximum(z, SLOPE * z).astype(BF16)


def kernel(
    state, surface, w1h, w2h, w3h, w4h, w5h, lith, off,
    out, flux,
    st, sfb, sf, w1, w2, w3, w4, w5t, lit, acc, mask, fr, fw, fl,
    rsend, rrecv, esend, erecv, ca, cb, oz, qb,
    load_sem, rs_sem, rr_sem, es_sem, er_sem, qs_sem, qr_sem,
):
    lat, lon = lax.axis_index("lat"), lax.axis_index("lon")
    core, quarter = lax.rem(lon, 2), lax.rem(lon, 4)

    def at(dlat, dlon):
        return (lat + dlat, lax.rem(lon + dlon + N_LON, N_LON))

    loads = [
        pltpu.make_async_copy(state.at[0 : 3 * FIELD], st.at[0 : 3 * FIELD], load_sem.at[0]),
        pltpu.make_async_copy(state.at[3 * FIELD : 8 * FIELD], st.at[3 * FIELD : 8 * FIELD], load_sem.at[1]),
        pltpu.make_async_copy(surface, sfb, load_sem.at[2]),
        pltpu.make_async_copy(lith, lit, load_sem.at[3]),
        pltpu.make_async_copy(w1h, w1, load_sem.at[4]),
        pltpu.make_async_copy(w5h, w5t, load_sem.at[5]),
        pltpu.make_async_copy(w2h, w2, load_sem.at[6]),
        pltpu.make_async_copy(w3h, w3, load_sem.at[7]),
        pltpu.make_async_copy(w4h, w4, load_sem.at[8]),
    ]
    for load in loads:
        load.start()

    barrier = pltpu.get_barrier_semaphore()

    def greet(dlat, dlon):
        pl.semaphore_signal(barrier, inc=1, device_id=at(dlat, dlon), device_id_type=MESH)

    for dlon in (-3, -2, -1, 1, 2, 3):
        greet(0, dlon)

    @pl.when(lat > 0)
    def _():
        for dlon in (-1, 0, 1):
            greet(-1, dlon)

    @pl.when(lat < N_LAT - 1)
    def _():
        for dlon in (-1, 0, 1):
            greet(1, dlon)

    loads[0].wait()
    sub3 = lax.broadcasted_iota(jnp.int32, (HC, ROWS, COLS), 1) < 4
    for ch in range(NCH):
        for f in range(3):
            x = st[f * FIELD + ch * LC * ROWS : f * FIELD + (ch + 1) * LC * ROWS].reshape(LC, ROWS, COLS)
            low, high = x[:HC], x[HC:]
            to_south = jnp.where(sub3, low, pltpu.roll(high, 4, 1))
            to_north = jnp.where(sub3, pltpu.roll(low, 4, 1), high)
            spot = slice(f * HC * ROWS, (f + 1) * HC * ROWS)
            rsend[0, ch, spot] = to_south.reshape(HC * ROWS, COLS).astype(BF16)
            rsend[1, ch, spot] = to_north.reshape(HC * ROWS, COLS).astype(BF16)
    lane2 = lax.broadcasted_iota(jnp.int32, (ROWS, COLS), 1)
    packed = []
    for f in range(3):
        for g in range(GROUPS):
            total = jnp.zeros((ROWS, COLS), F32)
            for kk in range(PER):
                row = (f * LEV + g * PER + kk) * ROWS
                total = jnp.where(lane2 // 8 == kk, pltpu.roll(st[row : row + ROWS], 4 + 8 * kk, 1), total)
            packed.append(total)
    esend[...] = jnp.concatenate(packed, axis=0).astype(BF16)

    neighbours = 6 + 3 * ((lat + N_LAT - 1) // N_LAT) + 3 * ((2 * N_LAT - 2 - lat) // N_LAT)
    pl.semaphore_wait(barrier, neighbours)

    def row_copy(side, ch):
        return pltpu.make_async_remote_copy(
            src_ref=rsend.at[side, ch], dst_ref=rrecv.at[side, ch],
            send_sem=rs_sem.at[side, ch], recv_sem=rr_sem.at[side, ch],
            device_id=at(2 * side - 1, 0), device_id_type=MESH,
        )

    def edge_copy(e):
        dlat, dlon = EDGES[e]
        place = EDGES.index((-dlat, -dlon))
        return pltpu.make_async_remote_copy(
            src_ref=esend, dst_ref=erecv.at[place],
            send_sem=es_sem.at[e], recv_sem=er_sem.at[place],
            device_id=at(dlat, dlon), device_id_type=MESH,
        )

    @pl.when(lat > 0)
    def _():
        edge_copy(2).start()
        edge_copy(3).start()

    @pl.when(lat < N_LAT - 1)
    def _():
        edge_copy(4).start()
        edge_copy(5).start()

    edge_copy(0).start()
    edge_copy(1).start()
    for ch in range(NCH):

        @pl.when(lat > 0)
        def _():
            row_copy(0, ch).start()

        @pl.when(lat < N_LAT - 1)
        def _():
            row_copy(1, ch).start()

    @pl.when(lat == 0)
    def _():
        rrecv[1] = jnp.zeros(rrecv.shape[1:], BF16)
        erecv[2] = jnp.zeros(erecv.shape[1:], BF16)
        erecv[3] = jnp.zeros(erecv.shape[1:], BF16)

    @pl.when(lat == N_LAT - 1)
    def _():
        rrecv[0] = jnp.zeros(rrecv.shape[1:], BF16)
        erecv[4] = jnp.zeros(erecv.shape[1:], BF16)
        erecv[5] = jnp.zeros(erecv.shape[1:], BF16)

    def block(n, slot):
        if isinstance(n, int) and n == OZ:
            return oz.at[slot]
        return qb.at[slot, pl.ds(n * CH, CH)]

    def send(n, flow, source, slot, dlon):
        return pltpu.make_async_remote_copy(
            src_ref=block(n, source), dst_ref=block(n, slot),
            send_sem=qs_sem.at[n, flow], recv_sem=qr_sem.at[n, slot],
            device_id=at(0, dlon), device_id_type=MESH,
        )

    def first_hops(n, act):
        @pl.when(core == 0)
        def _():
            act(send(n, 0, 0, 2, 2))
            act(send(n, 1, 0, 1, 1))

        @pl.when(core == 1)
        def _():
            act(send(n, 0, 0, 3, 3))

        @pl.when(quarter == 1)
        def _():
            act(send(n, 1, 0, 2, 2))

    def arrived(n, slot):
        send(n, 0, 0, slot, 1).wait_recv()

    def forward(n):
        @pl.when(core == 0)
        def _():
            arrived(n, 3)

        @pl.when(quarter == 2)
        def _():
            send(n, 2, 3, 2, -1).start()

        arrived(n, 2)

        @pl.when(core == 0)
        def _():
            send(n, 3, 2, 3, 1).start()

        @pl.when(core == 1)
        def _():
            send(n, 3, 2, 1, -1).start()

    def complete(n):
        arrived(n, 1)

        @pl.when(core == 1)
        def _():
            arrived(n, 3)

    def drain(n):
        first_hops(n, lambda copy: copy.wait_send())

        @pl.when(quarter == 2)
        def _():
            send(n, 2, 3, 2, -1).wait_send()

        @pl.when(core == 0)
        def _():
            send(n, 3, 2, 3, 1).wait_send()

        @pl.when(core == 1)
        def _():
            send(n, 3, 2, 1, -1).wait_send()

    loads[1].wait()
    for j in range(ROWS):
        oz[0, j] = st[pl.ds(7 * FIELD + j, LEV, stride=ROWS), :].astype(BF16)
    first_hops(OZ, lambda copy: copy.start())
    loads[2].wait()
    sf[...] = sfb[...].astype(F32)
    loads[3].wait()
    listed = lit[...]
    row_id = lax.broadcasted_iota(jnp.int32, (ROWS, COLS), 0)
    col_id = lax.broadcasted_iota(jnp.int32, (COLS, COLS), 0)
    in_row, in_col = [], []
    for r in range(ROWS):
        entry = listed[r : r + 1]
        in_row.append(jnp.where(jnp.broadcast_to(entry >> 7, (ROWS, COLS)) == row_id, 1.0, 0.0))
        in_col.append(jnp.where(jnp.broadcast_to(entry & 127, (COLS, COLS)) == col_id, 1.0, 0.0))
    mask[...] = nt(jnp.concatenate(in_row, 1).astype(BF16), jnp.concatenate(in_col, 1).astype(BF16))
    loads[4].wait()
    eye_c = eye(COLS)

    def static_rows(j, carry):
        tracers = st[pl.ds(DYN * ROWS + j, 8 * LEV - DYN, stride=ROWS), :]
        ground = sf[pl.ds(j, 76, stride=ROWS), :]
        x = jnp.concatenate([tracers, ground], axis=0).astype(BF16)
        xt = nt(eye_c, x).astype(BF16)
        spot = pl.ds(pl.multiple_of(j * COLS, COLS), COLS)
        acc[spot, :] = jnp.dot(xt, w1[DYN:NIN], preferred_element_type=F32)
        return carry

    lax.fori_loop(0, ROWS, static_rows, 0)
    loads[5].wait()

    @pl.when(lat > 0)
    def _():
        edge_copy(5).wait_recv()
        edge_copy(4).wait_recv()

    @pl.when(lat < N_LAT - 1)
    def _():
        edge_copy(3).wait_recv()
        edge_copy(2).wait_recv()

    edge_copy(1).wait_recv()
    edge_copy(0).wait_recv()
    edge_shape = (3 * GROUPS * ROWS, COLS)
    west_half = lax.broadcasted_iota(jnp.int32, edge_shape, 1) % 8 < 4
    north_half = lax.broadcasted_iota(jnp.int32, edge_shape, 0) % 8 < 4
    edge = [erecv[e].astype(F32) for e in range(6)]
    ca[...] = jnp.where(west_half, edge[0], edge[1])
    cb[...] = jnp.where(north_half, jnp.where(west_half, edge[4], edge[5]), jnp.where(west_half, edge[2], edge[3]))

    shape = (LC, ROWS, COLS)
    lane = lax.broadcasted_iota(jnp.int32, shape, 2)
    sub = lax.broadcasted_iota(jnp.int32, shape, 1)
    first_lane, last_lane, first_sub, last_sub = lane == 0, lane == COLS - 1, sub == 0, sub == ROWS - 1
    row_a = lat * ROWS + sub
    row_b = lat * ROWS + jnp.where(sub < 4, sub + ROWS, sub - ROWS)
    open_a = row_a < N_LAT * ROWS - 1
    open_b = jnp.logical_and(row_b >= 0, row_b < N_LAT * ROWS - 1)

    def swap(edge_mask, x, y):
        return jnp.where(edge_mask, y, x), jnp.where(edge_mask, x, y)

    def east(x, h):
        return swap(last_lane, pltpu.roll(x, COLS - 1, 2), pltpu.roll(h, COLS - 1, 2))

    def west(x, h):
        return swap(first_lane, pltpu.roll(x, 1, 2), pltpu.roll(h, 1, 2))

    def north(x, h):
        return swap(last_sub, pltpu.roll(x, ROWS - 1, 1), pltpu.roll(h, ROWS - 1, 1))

    def south(x, h):
        return swap(first_sub, pltpu.roll(x, 1, 1), pltpu.roll(h, 1, 1))

    def acoustic(ch, carry):
        @pl.when(lat > 0)
        def _():
            row_copy(1, ch).wait_recv()

        @pl.when(lat < N_LAT - 1)
        def _():
            row_copy(0, ch).wait_recv()

        half = lax.broadcasted_iota(jnp.int32, (HC, ROWS, COLS), 1) < 4
        quads = []
        for f in range(3):
            spot = pl.ds(pl.multiple_of(f * FIELD + ch * LC * ROWS, ROWS), LC * ROWS)
            a = st[spot, :].reshape(shape)
            rows = slice(f * HC * ROWS, (f + 1) * HC * ROWS)
            nn = rrecv[0, ch, rows].astype(F32).reshape(HC, ROWS, COLS)
            ss = rrecv[1, ch, rows].astype(F32).reshape(HC, ROWS, COLS)
            b = jnp.concatenate(
                [jnp.where(half, nn, pltpu.roll(ss, 4, 1)), jnp.where(half, pltpu.roll(nn, 4, 1), ss)], axis=0
            )
            sides = []
            for source in (ca, cb):
                pieces = []
                for g in range(LC // PER):
                    at_row = pl.multiple_of((f * GROUPS + ch * (LC // PER) + g) * ROWS, ROWS)
                    group = source[pl.ds(at_row, ROWS), :]
                    for kk in range(PER):
                        pieces.append(pltpu.roll(group, (COLS - 4 - 8 * kk) % COLS, 1).reshape(1, ROWS, COLS))
                sides.append(jnp.concatenate(pieces, axis=0))
            quads.append((a, b, sides[0], sides[1]))
        za, zb, zc, zd = quads[0]
        ma, mb, mc, md = quads[1]
        pa, pb, pc, pd = quads[2]
        ma, mc = jnp.where(open_a, ma, 0.0), jnp.where(open_a, mc, 0.0)
        mb, md = jnp.where(open_b, mb, 0.0), jnp.where(open_b, md, 0.0)
        zwa, zwc = west(za, zc)
        zwb, zwd = west(zb, zd)
        msa, msb = south(ma, mb)
        msc, msd = south(mc, md)
        da = COURANT * (za - zwa + ma - msa)
        db = COURANT * (zb - zwb + mb - msb)
        dc = COURANT * (zc - zwc + mc - msc)
        dd = COURANT * (zd - zwd + md - msd)
        sa, sb, sc, sd = pa, pb, pc, pd
        square = COURANT * COURANT
        for step in range(1, 5):
            ea, ec = east(sa, sc)
            wa, wc = west(sa, sc)
            na, nb = north(sa, sb)
            ga, gb = jnp.where(open_a, na - sa, 0.0), jnp.where(open_b, nb - sb, 0.0)
            gsa, gsb = south(ga, gb)
            new_pa = pa - da + square * (ea + wa - 2.0 * sa + ga - gsa)
            if step < 4:
                eb, ed = east(sb, sd)
                wb, wd = west(sb, sd)
                nc, nd = north(sc, sd)
                gc, gd = jnp.where(open_a, nc - sc, 0.0), jnp.where(open_b, nd - sd, 0.0)
                gsc, gsd = south(gc, gd)
                pb = pb - db + square * (eb + wb - 2.0 * sb + gb - gsb)
                pc = pc - dc + square * (ec + wc - 2.0 * sc + gc - gsc)
                if step < 3:
                    pd = pd - dd + square * (ed + wd - 2.0 * sd + gd - gsd)
                pa = new_pa
                sa, sb, sc, sd = sa + pa, sb + pb, sc + pc, sd + pd
            else:
                pa = new_pa
        za = za - COURANT * (ea - sa)
        zc = zc - COURANT * (ec - sc)
        ma = jnp.where(open_a, ma - COURANT * ga, 0.0)
        z_west, _ = west(za, zc)
        share = (0.5 + 0.45 * jnp.tanh(za)).reshape(LC * ROWS, COLS)
        share_west = (0.5 + 0.45 * jnp.tanh(z_west)).reshape(LC * ROWS, COLS)
        for f, value in enumerate((za, ma, pa)):
            spot = pl.ds(pl.multiple_of(f * FIELD + ch * LC * ROWS, ROWS), LC * ROWS)
            st[spot, :] = value.reshape(LC * ROWS, COLS)
        out[pl.ds(pl.multiple_of(2 * FIELD + ch * LC * ROWS, ROWS), LC * ROWS), :] = pa.reshape(LC * ROWS, COLS)
        for f in range(4):
            spot = pl.ds(pl.multiple_of(f * FIELD + ch * LC * ROWS, ROWS), LC * ROWS)
            fr[spot, :] = share
            fw[spot, :] = share_west
        return carry

    lax.fori_loop(0, NCH, acoustic, 0)

    for load in loads[6:]:
        load.wait()

    def network(n, carry):
        xs = []
        for r in range(CH):
            x = st[pl.ds(n * CH + r, DYN, stride=ROWS), :].astype(BF16)
            xs.append(nt(eye_c, x).astype(BF16))
        xt = jnp.concatenate(xs, axis=0)
        spot = pl.ds(pl.multiple_of(n * CH * COLS, COLS), CH * COLS)
        h = leaky(acc[spot, :] + jnp.dot(xt, w1[0:DYN], preferred_element_type=F32))
        for w in (w2, w3, w4):
            h = leaky(jnp.dot(h, w[...], preferred_element_type=F32))
        y = nt(w5t[...], h)
        for r in range(CH):
            j = n * CH + r
            t = jnp.where(jnp.broadcast_to(mask[pl.ds(j, 1), :], (NOUT, COLS)) > 0.5, y[:, r * COLS : (r + 1) * COLS], 0.0)
            out[pl.ds(j, 2 * LEV, stride=ROWS), :] = st[pl.ds(j, 2 * LEV, stride=ROWS), :] + STEP * t[0 : 2 * LEV]
            q = st[pl.ds(3 * FIELD + j, 4 * LEV, stride=ROWS), :] + STEP * t[2 * LEV : 6 * LEV]
            qb[0, j] = q.astype(BF16)
            fl[pl.ds(j, 8, stride=ROWS), :] = t[6 * LEV :]
        first_hops(n, lambda copy: copy.start())
        return carry

    lax.fori_loop(0, NB, network, 0)
    flux[...] = fl[...].astype(BF16)

    def advect(j, ref, count, base):
        offset = off[j]
        tiles, cells = offset >> 7, offset & 127
        tile_shape = (count, COLS)
        where = lax.broadcasted_iota(jnp.int32, tile_shape, 1)
        parts = [ref[slot, j].astype(F32) for slot in range(4)]

        def pick(cut):
            d = tiles + jnp.where(where >= cut, 1, 0)
            return jnp.where(d == 0, parts[0], jnp.where(d == 1, parts[1], jnp.where(d == 2, parts[2], parts[3])))

        near = pltpu.roll(pick(COLS - cells), cells, 1)
        far = pltpu.roll(pick(COLS - 1 - cells), (cells + 1) & 127, 1)
        spot = pl.ds(j, count, stride=ROWS)
        value = (1.0 - fr[spot, :]) * near + fw[spot, :] * far
        out[pl.ds(base * FIELD + j, count, stride=ROWS), :] = value

    forward(OZ)

    def tracer_block(n, carry):
        forward(n)
        complete(n)
        for r in range(CH):
            advect(n * CH + r, qb, 4 * LEV, 3)
        return carry

    complete(OZ)

    def ozone_row(j, carry):
        advect(j, oz, LEV, 7)
        return carry

    lax.fori_loop(0, ROWS, ozone_row, 0)
    lax.fori_loop(0, NB, tracer_block, 0)

    @pl.when(lat > 0)
    def _():
        edge_copy(2).wait_send()
        edge_copy(3).wait_send()

    @pl.when(lat < N_LAT - 1)
    def _():
        edge_copy(4).wait_send()
        edge_copy(5).wait_send()

    edge_copy(0).wait_send()
    edge_copy(1).wait_send()
    for ch in range(NCH):

        @pl.when(lat > 0)
        def _():
            row_copy(0, ch).wait_send()

        @pl.when(lat < N_LAT - 1)
        def _():
            row_copy(1, ch).wait_send()

    drain(OZ)

    def drain_block(n, carry):
        drain(n)
        return carry

    lax.fori_loop(0, NB, drain_block, 0)


def on_device(state, surface, layer_one, layer_two, layer_three, layer_four, layer_five, lit_columns, row_offset):
    fields = state.shape[0]
    any_spec = pl.BlockSpec(memory_space=pl.ANY)
    vmem_spec = pl.BlockSpec(memory_space=pltpu.VMEM)
    dma = pltpu.SemaphoreType.DMA
    new_state, surface_flux = pl.pallas_call(
        kernel,
        out_shape=(
            jax.ShapeDtypeStruct((fields * FIELD, COLS), F32),
            jax.ShapeDtypeStruct((8 * ROWS, COLS), BF16),
        ),
        in_specs=[any_spec] * 8 + [pl.BlockSpec(memory_space=pltpu.SMEM)],
        out_specs=(vmem_spec, vmem_spec),
        scratch_shapes=[
            pltpu.VMEM((fields * FIELD, COLS), F32),
            pltpu.VMEM((76 * ROWS, COLS), BF16),
            pltpu.VMEM((76 * ROWS, COLS), F32),
            pltpu.VMEM((NIN, H1), BF16),
            pltpu.VMEM((H1, H2), BF16),
            pltpu.VMEM((H2, H3), BF16),
            pltpu.VMEM((H3, H4), BF16),
            pltpu.VMEM((NOUT, H4), BF16),
            pltpu.VMEM((ROWS, COLS), jnp.int32),
            pltpu.VMEM((ROWS * COLS, H1), F32),
            pltpu.VMEM((ROWS, COLS), F32),
            pltpu.VMEM((4 * FIELD, COLS), F32),
            pltpu.VMEM((4 * FIELD, COLS), F32),
            pltpu.VMEM((8 * ROWS, COLS), F32),
            pltpu.VMEM((2, NCH, 3 * HC * ROWS, COLS), BF16),
            pltpu.VMEM((2, NCH, 3 * HC * ROWS, COLS), BF16),
            pltpu.VMEM((3 * GROUPS * ROWS, COLS), BF16),
            pltpu.VMEM((6, 3 * GROUPS * ROWS, COLS), BF16),
            pltpu.VMEM((3 * GROUPS * ROWS, COLS), F32),
            pltpu.VMEM((3 * GROUPS * ROWS, COLS), F32),
            pltpu.VMEM((4, ROWS, LEV, COLS), BF16),
            pltpu.VMEM((4, ROWS, 4 * LEV, COLS), BF16),
            dma((9,)),
            dma((2, NCH)),
            dma((2, NCH)),
            dma((6,)),
            dma((6,)),
            dma((NB + 1, 4)),
            dma((NB + 1, 4)),
        ],
        compiler_params=pltpu.CompilerParams(
            collective_id=0, has_side_effects=True, vmem_limit_bytes=56 * 1024 * 1024
        ),
    )(
        state.reshape(fields * FIELD, COLS),
        surface.reshape(76 * ROWS, COLS),
        layer_one, layer_two, layer_three, layer_four, layer_five.T,
        lit_columns.reshape(ROWS, COLS),
        row_offset,
    )
    return new_state.reshape(fields, LEV, ROWS, COLS), surface_flux.reshape(8, ROWS, COLS)


def solution(mesh):
    in_specs = (
        P(None, None, "lat", "lon"), P(None, "lat", "lon"), P(), P(), P(), P(), P(), P("lat", "lon", None), P("lat"),
    )
    out_specs = (P(None, None, "lat", "lon"), P(None, "lat", "lon"))
    return jax.shard_map(on_device, mesh=mesh, in_specs=in_specs, out_specs=out_specs, check_vma=False)
```

profile of v0, /device:TPU:23, one launch (start us, length us, event | category | flops | bytes accessed | tf_op | source)
XLA Modules:
  0.0 41.4 jit_solution(13273814655887099050)
XLA Ops:
  0.6 37.2 %shard_map.104 = (f32[3840,128]{1,0:T(8,128)}, bf16[64,128]{1,0:T(8,128)(2,1)}) custom-call(f32[3840,128]{1,0:T(8,128)} %bitcast.6, bf16[608,128]{1,0:T(8,128)(2,1)} %bitcast.9, bf16[556,768]{1,0:T(8,128)(2,1)} %w1h.1, bf16[768,640]{1,0:T(8,128)(2,1)} %w2h.1, bf16[640,512]{1,0:T(8,128)(2,1)} %w3h.1, bf16[512,640]{1,0:T(8,128)(2,1)} %w4h.1, ...), custom_call_target="tpu_custom_call" | custom-call | tf_op jit(solution)/shard_map/pallas_call | solution.py:492
  37.8 0.0 copy-start
  37.8 3.0 %copy.13 = f32[8,60,8,128]{3,2,1,0:T(8,128)} copy(f32[8,60,8,128]{3,2,1,0:T(8,128)} %bitcast.7) | data formatting | bytes 3932160
  40.8 0.0 copy-done
  40.8 0.6 %copy.14 = bf16[8,8,128]{2,1,0:T(8,128)(2,1)} copy(bf16[8,8,128]{2,1,0:T(8,128)(2,1)S(1)} %bitcast.10) | data formatting | bytes 32768
Async XLA Ops:
  37.8 3.0 %copy-start = (bf16[64,128]{1,0:T(8,128)(2,1)S(1)}, bf16[64,128]{1,0:T(8,128)(2,1)}, u32[]{:S(2)}) copy-start(bf16[64,128]{1,0:T(8,128)(2,1)} %get-tuple-element.5) | copy-start | bytes 49156
where the time goes:
time: 41.6 us; the launch traced here: 41.4 us
  Pallas kernels  37.2 us (89%)
  local copies, waits for them, and re-layouts  3.57 us (9%)
  between operations  0.65 us (2%)
    pallas_call x1, Pallas kernels, on_device(): pl.pallas_call(kernel, out_shape=(jax.ShapeDtypeStruct((fields * FIELD, C...  37.2 us
    unnamed x4, local copies, waits for them, and re-layouts  3.57 us

commit v1 on v0

--- a/solution.py
+++ b/solution.py
@@ -484,6 +484,17 @@
     lax.fori_loop(0, NB, drain_block, 0)
 
 
+def place(state, flux, state_out, flux_out, sem):
+    copies = [pltpu.make_async_copy(flux, flux_out, sem.at[4])]
+    for part in range(4):
+        spot = slice(part * 2 * FIELD, (part + 1) * 2 * FIELD)
+        copies.append(pltpu.make_async_copy(state.at[spot], state_out.at[spot], sem.at[part]))
+    for copy in copies:
+        copy.start()
+    for copy in copies:
+        copy.wait()
+
+
 def on_device(state, surface, layer_one, layer_two, layer_three, layer_four, layer_five, lit_columns, row_offset):
     fields = state.shape[0]
     any_spec = pl.BlockSpec(memory_space=pl.ANY)
@@ -492,8 +503,8 @@
     new_state, surface_flux = pl.pallas_call(
         kernel,
         out_shape=(
-            jax.ShapeDtypeStruct((fields * FIELD, COLS), F32),
-            jax.ShapeDtypeStruct((8 * ROWS, COLS), BF16),
+            pltpu.VMEM((fields * FIELD, COLS), F32),
+            pltpu.VMEM((8 * ROWS, COLS), BF16),
         ),
         in_specs=[any_spec] * 8 + [pl.BlockSpec(memory_space=pltpu.SMEM)],
         out_specs=(vmem_spec, vmem_spec),
@@ -538,6 +549,16 @@
         lit_columns.reshape(ROWS, COLS),
         row_offset,
     )
+    new_state, surface_flux = pl.pallas_call(
+        place,
+        out_shape=(
+            jax.ShapeDtypeStruct((fields * FIELD, COLS), F32),
+            jax.ShapeDtypeStruct((8 * ROWS, COLS), BF16),
+        ),
+        in_specs=[vmem_spec, vmem_spec],
+        out_specs=(any_spec, any_spec),
+        scratch_shapes=[dma((5,))],
+    )(pltpu.with_memory_space_constraint(new_state, pltpu.VMEM), pltpu.with_memory_space_constraint(surface_flux, pltpu.VMEM))
     return new_state.reshape(fields, LEV, ROWS, COLS), surface_flux.reshape(8, ROWS, COLS)
 
 

time: 41.6 us -> 37.9 us (0.911)
  local copies, waits for them, and re-layouts: 3.57 us -> 0 us
    unnamed x4 -> x0, local copies, waits for them, and re-layouts: 3.57 us -> none
    pallas_call x1 -> x2, Pallas kernels: 37.2 us -> 37.2 us  [the longest x1 35.9 us: on_device(): pl.pallas_call(kernel, out_shape=(pltpu.VMEM((fields * FIELD, COLS), F32)...]
where the time goes in v1:
time: 37.9 us; the launch traced here: 37.8 us
  Pallas kernels  37.2 us (98%)
  between operations  0.64 us (2%)
    pallas_call x1, Pallas kernels, on_device(): pl.pallas_call(kernel, out_shape=(pltpu.VMEM((fields * FIELD, COLS), F32)...  35.9 us
    pallas_call x1, Pallas kernels, on_device(): pl.pallas_call(place, out_shape=(jax.ShapeDtypeStruct((fields * FIELD, CO...  1.31 us

profile of v1, /device:TPU:23, one launch (start us, length us, event | category | flops | bytes accessed | tf_op | source)
XLA Modules:
  0.0 37.8 jit_solution(4111183235998069425)
XLA Ops:
  0.6 35.9 %shard_map.104 = (f32[3840,128]{1,0:T(8,128)S(1)}, bf16[64,128]{1,0:T(8,128)(2,1)S(1)}) custom-call(f32[3840,128]{1,0:T(8,128)} %bitcast.6, bf16[608,128]{1,0:T(8,128)(2,1)} %bitcast.8, bf16[556,768]{1,0:T(8,128)(2,1)} %w1h.1, bf16[768,640]{1,0:T(8,128)(2,1)} %w2h.1, bf16[640,512]{1,0:T(8,128)(2,1)} %w3h.1, bf16[512,640]{1,0:T(8,128)(2,1)} %w4h.1, ...), custom_call_target="tpu_custom_call" | custom-call | tf_op jit(solution)/shard_map/pallas_call | solution.py:503
  36.5 1.3 %shard_map.105 = (f32[3840,128]{1,0:T(8,128)}, bf16[64,128]{1,0:T(8,128)(2,1)}) custom-call(f32[3840,128]{1,0:T(8,128)S(1)} %get-tuple-element.6.state, bf16[64,128]{1,0:T(8,128)(2,1)S(1)} %get-tuple-element.7.flux), custom_call_target="tpu_custom_call" | custom-call | tf_op jit(solution)/shard_map/pallas_call | solution.py:552

commit v2 on v1

--- a/solution.py
+++ b/solution.py
@@ -19,16 +19,17 @@
 NIN, NOUT = 556, 368
 H1, H2, H3, H4 = 768, 640, 512, 640
 
-LC = 20
+LC = 30
 NCH = LEV // LC
-HC = LC // 2
-PER = 10
+PER = 15
 GROUPS = LEV // PER
+EROWS = 3 * GROUPS * ROWS
 CH = 2
 NB = ROWS // CH
-OZ = NB
-
-EDGES = ((0, -1), (0, 1), (-1, -1), (-1, 1), (1, -1), (1, 1))
+OZ = ROWS
+
+AROUND = ((0, -1), (0, 1), (-1, 0), (1, 0), (-1, -1), (-1, 1), (1, -1), (1, 1))
+A1, B1, ZA, ZB, ZF = 0, 4, 7, 8, 9
 
 
 def nt(a, b):
@@ -47,7 +48,7 @@
     state, surface, w1h, w2h, w3h, w4h, w5h, lith, off,
     out, flux,
     st, sfb, sf, w1, w2, w3, w4, w5t, lit, acc, mask, fr, fw, fl,
-    rsend, rrecv, esend, erecv, ca, cb, oz, qb,
+    own_div, rsend, rrecv, own_edge, esend, hsend, erecv, hrecv, give, oz, qb,
     load_sem, rs_sem, rr_sem, es_sem, er_sem, qs_sem, qr_sem,
 ):
     lat, lon = lax.axis_index("lat"), lax.axis_index("lon")
@@ -89,16 +90,23 @@
             greet(1, dlon)
 
     loads[0].wait()
-    sub3 = lax.broadcasted_iota(jnp.int32, (HC, ROWS, COLS), 1) < 4
+    shape = (LC, ROWS, COLS)
+    lane = lax.broadcasted_iota(jnp.int32, shape, 2)
+    sub = lax.broadcasted_iota(jnp.int32, shape, 1)
     for ch in range(NCH):
-        for f in range(3):
-            x = st[f * FIELD + ch * LC * ROWS : f * FIELD + (ch + 1) * LC * ROWS].reshape(LC, ROWS, COLS)
-            low, high = x[:HC], x[HC:]
-            to_south = jnp.where(sub3, low, pltpu.roll(high, 4, 1))
-            to_north = jnp.where(sub3, pltpu.roll(low, 4, 1), high)
-            spot = slice(f * HC * ROWS, (f + 1) * HC * ROWS)
-            rsend[0, ch, spot] = to_south.reshape(HC * ROWS, COLS).astype(BF16)
-            rsend[1, ch, spot] = to_north.reshape(HC * ROWS, COLS).astype(BF16)
+        z, m, p = (
+            st[f * FIELD + ch * LC * ROWS : f * FIELD + (ch + 1) * LC * ROWS].reshape(shape) for f in range(3)
+        )
+        m = jnp.where(lat * ROWS + sub < N_LAT * ROWS - 1, m, 0.0)
+        m_south = pltpu.roll(m, 1, 1)
+        z_west = jnp.where(lane == 0, 0.0, pltpu.roll(z, 1, 2))
+        d = COURANT * (z - z_west + m - jnp.where(sub == 0, 0.0, m_south))
+        own_div[ch * LC * ROWS : (ch + 1) * LC * ROWS] = d.reshape(LC * ROWS, COLS)
+        d_turned = pltpu.roll(d, 4, 1)
+        to_south = jnp.where(sub < 4, p, d_turned)
+        to_north = jnp.where(sub >= 4, p, jnp.where(sub >= 1, d_turned, m_south))
+        rsend[0, ch] = to_south.reshape(LC * ROWS, COLS).astype(BF16)
+        rsend[1, ch] = to_north.reshape(LC * ROWS, COLS).astype(BF16)
     lane2 = lax.broadcasted_iota(jnp.int32, (ROWS, COLS), 1)
     packed = []
     for f in range(3):
@@ -108,7 +116,14 @@
                 row = (f * LEV + g * PER + kk) * ROWS
                 total = jnp.where(lane2 // 8 == kk, pltpu.roll(st[row : row + ROWS], 4 + 8 * kk, 1), total)
             packed.append(total)
-    esend[...] = jnp.concatenate(packed, axis=0).astype(BF16)
+    own_edge[...] = jnp.concatenate(packed, axis=0)
+    edges = own_edge[...]
+    esend[...] = edges.astype(BF16)
+    edges = edges.reshape(2, 3 * GROUPS // 2, ROWS, COLS)
+    low, high = edges[0], edges[1]
+    half = lax.broadcasted_iota(jnp.int32, low.shape, 1) < 4
+    hsend[0] = jnp.where(half, low, pltpu.roll(high, 4, 1)).reshape(EROWS // 2, COLS).astype(BF16)
+    hsend[1] = jnp.where(half, pltpu.roll(low, 4, 1), high).reshape(EROWS // 2, COLS).astype(BF16)
 
     neighbours = 6 + 3 * ((lat + N_LAT - 1) // N_LAT) + 3 * ((2 * N_LAT - 2 - lat) // N_LAT)
     pl.semaphore_wait(barrier, neighbours)
@@ -121,26 +136,35 @@
         )
 
     def edge_copy(e):
-        dlat, dlon = EDGES[e]
-        place = EDGES.index((-dlat, -dlon))
+        dlat, dlon = AROUND[e]
+        place = AROUND.index((-dlat, -dlon))
+        if dlat == 0:
+            source, target = esend, erecv.at[place]
+        else:
+            source, target = hsend.at[(dlat + 1) // 2], hrecv.at[place - 2]
         return pltpu.make_async_remote_copy(
-            src_ref=esend, dst_ref=erecv.at[place],
+            src_ref=source, dst_ref=target,
             send_sem=es_sem.at[e], recv_sem=er_sem.at[place],
             device_id=at(dlat, dlon), device_id_type=MESH,
         )
 
-    @pl.when(lat > 0)
-    def _():
-        edge_copy(2).start()
-        edge_copy(3).start()
-
-    @pl.when(lat < N_LAT - 1)
-    def _():
-        edge_copy(4).start()
-        edge_copy(5).start()
-
-    edge_copy(0).start()
-    edge_copy(1).start()
+    to_south, to_north = (2, 4, 5), (3, 6, 7)
+
+    def all_edges(act):
+        @pl.when(lat > 0)
+        def _():
+            for e in to_south:
+                act(edge_copy(e))
+
+        @pl.when(lat < N_LAT - 1)
+        def _():
+            for e in to_north:
+                act(edge_copy(e))
+
+        act(edge_copy(0))
+        act(edge_copy(1))
+
+    all_edges(lambda copy: copy.start())
     for ch in range(NCH):
 
         @pl.when(lat > 0)
@@ -154,19 +178,19 @@
     @pl.when(lat == 0)
     def _():
         rrecv[1] = jnp.zeros(rrecv.shape[1:], BF16)
-        erecv[2] = jnp.zeros(erecv.shape[1:], BF16)
-        erecv[3] = jnp.zeros(erecv.shape[1:], BF16)
+        for e in to_south:
+            hrecv[e - 2] = jnp.zeros(hrecv.shape[1:], BF16)
 
     @pl.when(lat == N_LAT - 1)
     def _():
         rrecv[0] = jnp.zeros(rrecv.shape[1:], BF16)
-        erecv[4] = jnp.zeros(erecv.shape[1:], BF16)
-        erecv[5] = jnp.zeros(erecv.shape[1:], BF16)
+        for e in to_north:
+            hrecv[e - 2] = jnp.zeros(hrecv.shape[1:], BF16)
 
     def block(n, slot):
         if isinstance(n, int) and n == OZ:
             return oz.at[slot]
-        return qb.at[slot, pl.ds(n * CH, CH)]
+        return qb.at[slot, n]
 
     def send(n, flow, source, slot, dlon):
         return pltpu.make_async_remote_copy(
@@ -264,48 +288,98 @@
     lax.fori_loop(0, ROWS, static_rows, 0)
     loads[5].wait()
 
+    def edge_arrival(place):
+        dlat, dlon = AROUND[place]
+        if dlat == 0:
+            source, target = esend, erecv.at[place]
+        else:
+            source, target = hsend.at[0], hrecv.at[place - 2]
+        return pltpu.make_async_remote_copy(
+            src_ref=source, dst_ref=target, send_sem=es_sem.at[place], recv_sem=er_sem.at[place],
+            device_id=at(dlat, dlon), device_id_type=MESH,
+        )
+
     @pl.when(lat > 0)
     def _():
-        edge_copy(5).wait_recv()
-        edge_copy(4).wait_recv()
+        for e in to_south:
+            edge_arrival(e).wait_recv()
 
     @pl.when(lat < N_LAT - 1)
     def _():
-        edge_copy(3).wait_recv()
-        edge_copy(2).wait_recv()
-
-    edge_copy(1).wait_recv()
-    edge_copy(0).wait_recv()
-    edge_shape = (3 * GROUPS * ROWS, COLS)
-    west_half = lax.broadcasted_iota(jnp.int32, edge_shape, 1) % 8 < 4
-    north_half = lax.broadcasted_iota(jnp.int32, edge_shape, 0) % 8 < 4
-    edge = [erecv[e].astype(F32) for e in range(6)]
-    ca[...] = jnp.where(west_half, edge[0], edge[1])
-    cb[...] = jnp.where(north_half, jnp.where(west_half, edge[4], edge[5]), jnp.where(west_half, edge[2], edge[3]))
-
-    shape = (LC, ROWS, COLS)
-    lane = lax.broadcasted_iota(jnp.int32, shape, 2)
-    sub = lax.broadcasted_iota(jnp.int32, shape, 1)
-    first_lane, last_lane, first_sub, last_sub = lane == 0, lane == COLS - 1, sub == 0, sub == ROWS - 1
-    row_a = lat * ROWS + sub
-    row_b = lat * ROWS + jnp.where(sub < 4, sub + ROWS, sub - ROWS)
-    open_a = row_a < N_LAT * ROWS - 1
-    open_b = jnp.logical_and(row_b >= 0, row_b < N_LAT * ROWS - 1)
-
-    def swap(edge_mask, x, y):
-        return jnp.where(edge_mask, y, x), jnp.where(edge_mask, x, y)
-
-    def east(x, h):
-        return swap(last_lane, pltpu.roll(x, COLS - 1, 2), pltpu.roll(h, COLS - 1, 2))
-
-    def west(x, h):
-        return swap(first_lane, pltpu.roll(x, 1, 2), pltpu.roll(h, 1, 2))
-
-    def north(x, h):
-        return swap(last_sub, pltpu.roll(x, ROWS - 1, 1), pltpu.roll(h, ROWS - 1, 1))
-
-    def south(x, h):
-        return swap(first_sub, pltpu.roll(x, 1, 1), pltpu.roll(h, 1, 1))
+        for e in to_north:
+            edge_arrival(e).wait_recv()
+
+    edge_arrival(0).wait_recv()
+    edge_arrival(1).wait_recv()
+
+    strip_shape = (2 * GROUPS, ROWS, COLS)
+    s_lane = lax.broadcasted_iota(jnp.int32, strip_shape, 2) % 8
+    s_sub = lax.broadcasted_iota(jnp.int32, strip_shape, 1)
+    group_shape = (3 * GROUPS, ROWS, COLS)
+    first_half = lax.broadcasted_iota(jnp.int32, group_shape, 2) % 8 < 4
+
+    def opened(sub):
+        row_a = lat * ROWS + sub
+        row_b = lat * ROWS + jnp.where(sub < 4, sub + ROWS, sub - ROWS)
+        return row_a < N_LAT * ROWS - 1, jnp.logical_and(row_b >= 0, row_b < N_LAT * ROWS - 1)
+
+    def beyond(north_place, south_place):
+        nn = hrecv[north_place - 2].astype(F32).reshape(half.shape)
+        ss = hrecv[south_place - 2].astype(F32).reshape(half.shape)
+        return jnp.concatenate(
+            [jnp.where(half, nn, pltpu.roll(ss, 4, 1)), jnp.where(half, pltpu.roll(nn, 4, 1), ss)], axis=0
+        )
+
+    def strips(west_edge, middle, east_edge):
+        on_east, on_west = jnp.where(first_half, middle, east_edge), jnp.where(first_half, west_edge, middle)
+        return [
+            jnp.concatenate([on_east[f * GROUPS : (f + 1) * GROUPS], on_west[f * GROUPS : (f + 1) * GROUPS]], axis=0)
+            for f in range(3)
+        ]
+
+    za, ma, pa = strips(
+        erecv[0].astype(F32).reshape(group_shape), own_edge[...].reshape(group_shape), erecv[1].astype(F32).reshape(group_shape)
+    )
+    zb, mb, pb = strips(beyond(6, 4), beyond(3, 2), beyond(7, 5))
+
+    def turn(x, steps):
+        return pltpu.roll(x, steps % COLS, 2)
+
+    def north(sub, x, y):
+        x, y = pltpu.roll(x, ROWS - 1, 1), pltpu.roll(y, ROWS - 1, 1)
+        return jnp.where(sub == ROWS - 1, y, x), jnp.where(sub == ROWS - 1, x, y)
+
+    def south(sub, x, y):
+        x, y = pltpu.roll(x, 1, 1), pltpu.roll(y, 1, 1)
+        return jnp.where(sub == 0, y, x), jnp.where(sub == 0, x, y)
+
+    def hand(index, value):
+        merged = jnp.where(s_lane[:GROUPS] == 2, turn(value[:GROUPS], -2), value[GROUPS:])
+        give[index] = merged.reshape(GROUPS * ROWS, COLS)
+
+    square = COURANT * COURANT
+    open_a, open_b = opened(s_sub)
+    ma, mb = jnp.where(open_a, ma, 0.0), jnp.where(open_b, mb, 0.0)
+    msa, msb = south(s_sub, ma, mb)
+    da = COURANT * (za - turn(za, 1) + ma - msa)
+    db = COURANT * (zb - turn(zb, 1) + mb - msb)
+    hand(ZA, COURANT * za)
+    hand(ZB, COURANT * zb)
+    sa, sb = pa, pb
+    for step in range(4):
+        hand(A1 + step, sa)
+        if step < 3:
+            hand(B1 + step, sb)
+            na, nb = north(s_sub, sa, sb)
+            ga, gb = jnp.where(open_a, na - sa, 0.0), jnp.where(open_b, nb - sb, 0.0)
+            gsa, gsb = south(s_sub, ga, gb)
+            pa = pa - da + square * (turn(sa, -1) + turn(sa, 1) - 2.0 * sa + ga - gsa)
+            pb = pb - db + square * (turn(sb, -1) + turn(sb, 1) - 2.0 * sb + gb - gsb)
+            sa, sb = sa + pa, sb + pb
+    hand(ZF, za - COURANT * (turn(sa, -1) - sa))
+
+    open_a, open_b = opened(sub)
+    first_lane, last_lane = lane == 0, lane == COLS - 1
 
     def acoustic(ch, carry):
         @pl.when(lat > 0)
@@ -316,77 +390,55 @@
         def _():
             row_copy(0, ch).wait_recv()
 
-        half = lax.broadcasted_iota(jnp.int32, (HC, ROWS, COLS), 1) < 4
-        quads = []
-        for f in range(3):
-            spot = pl.ds(pl.multiple_of(f * FIELD + ch * LC * ROWS, ROWS), LC * ROWS)
-            a = st[spot, :].reshape(shape)
-            rows = slice(f * HC * ROWS, (f + 1) * HC * ROWS)
-            nn = rrecv[0, ch, rows].astype(F32).reshape(HC, ROWS, COLS)
-            ss = rrecv[1, ch, rows].astype(F32).reshape(HC, ROWS, COLS)
-            b = jnp.concatenate(
-                [jnp.where(half, nn, pltpu.roll(ss, 4, 1)), jnp.where(half, pltpu.roll(nn, 4, 1), ss)], axis=0
-            )
-            sides = []
-            for source in (ca, cb):
-                pieces = []
-                for g in range(LC // PER):
-                    at_row = pl.multiple_of((f * GROUPS + ch * (LC // PER) + g) * ROWS, ROWS)
-                    group = source[pl.ds(at_row, ROWS), :]
-                    for kk in range(PER):
-                        pieces.append(pltpu.roll(group, (COLS - 4 - 8 * kk) % COLS, 1).reshape(1, ROWS, COLS))
-                sides.append(jnp.concatenate(pieces, axis=0))
-            quads.append((a, b, sides[0], sides[1]))
-        za, zb, zc, zd = quads[0]
-        ma, mb, mc, md = quads[1]
-        pa, pb, pc, pd = quads[2]
-        ma, mc = jnp.where(open_a, ma, 0.0), jnp.where(open_a, mc, 0.0)
-        mb, md = jnp.where(open_b, mb, 0.0), jnp.where(open_b, md, 0.0)
-        zwa, zwc = west(za, zc)
-        zwb, zwd = west(zb, zd)
-        msa, msb = south(ma, mb)
-        msc, msd = south(mc, md)
-        da = COURANT * (za - zwa + ma - msa)
-        db = COURANT * (zb - zwb + mb - msb)
-        dc = COURANT * (zc - zwc + mc - msc)
-        dd = COURANT * (zd - zwd + md - msd)
-        sa, sb, sc, sd = pa, pb, pc, pd
-        square = COURANT * COURANT
-        for step in range(1, 5):
-            ea, ec = east(sa, sc)
-            wa, wc = west(sa, sc)
-            na, nb = north(sa, sb)
+        def spot_of(f):
+            return pl.ds(pl.multiple_of(f * FIELD + ch * LC * ROWS, ROWS), LC * ROWS)
+
+        def given(index):
+            pieces = []
+            for g in range(LC // PER):
+                group = give[index, pl.ds(pl.multiple_of((ch * (LC // PER) + g) * ROWS, ROWS), ROWS), :]
+                for kk in range(PER):
+                    pieces.append(pltpu.roll(group, (COLS - 3 - 8 * kk) % COLS, 1).reshape(1, ROWS, COLS))
+            return jnp.concatenate(pieces, axis=0)
+
+        def sides(x, other):
+            return jnp.where(last_lane, other, turn(x, -1)) + jnp.where(first_lane, other, turn(x, 1))
+
+        from_north = rrecv[0, ch].astype(F32).reshape(shape)
+        from_south = rrecv[1, ch].astype(F32).reshape(shape)
+        pb = jnp.where(sub < 4, from_north, from_south)
+        db = pltpu.roll(jnp.where(sub < 4, from_south, from_north), 4, 1)
+        ma = jnp.where(open_a, st[spot_of(1), :].reshape(shape), 0.0)
+        db = db - jnp.where(first_lane, given(ZB), 0.0) - jnp.where(sub == 0, COURANT * pltpu.roll(ma, 1, 1), 0.0)
+        da = own_div[spot_of(0), :].reshape(shape)
+        da = da - jnp.where(first_lane, given(ZA), 0.0) - jnp.where(sub == 0, COURANT * from_south, 0.0)
+        pa = st[spot_of(2), :].reshape(shape)
+        sa, sb = pa, pb
+        for step in range(4):
+            na, nb = north(sub, sa, sb)
             ga, gb = jnp.where(open_a, na - sa, 0.0), jnp.where(open_b, nb - sb, 0.0)
-            gsa, gsb = south(ga, gb)
-            new_pa = pa - da + square * (ea + wa - 2.0 * sa + ga - gsa)
-            if step < 4:
-                eb, ed = east(sb, sd)
-                wb, wd = west(sb, sd)
-                nc, nd = north(sc, sd)
-                gc, gd = jnp.where(open_a, nc - sc, 0.0), jnp.where(open_b, nd - sd, 0.0)
-                gsc, gsd = south(gc, gd)
-                pb = pb - db + square * (eb + wb - 2.0 * sb + gb - gsb)
-                pc = pc - dc + square * (ec + wc - 2.0 * sc + gc - gsc)
-                if step < 3:
-                    pd = pd - dd + square * (ed + wd - 2.0 * sd + gd - gsd)
-                pa = new_pa
-                sa, sb, sc, sd = sa + pa, sb + pb, sc + pc, sd + pd
+            gsa, gsb = south(sub, ga, gb)
+            other = given(A1 + step)
+            if step == 3:
+                ea = jnp.where(last_lane, other, turn(sa, -1))
+                across = ea + jnp.where(first_lane, other, turn(sa, 1))
             else:
-                pa = new_pa
-        za = za - COURANT * (ea - sa)
-        zc = zc - COURANT * (ec - sc)
+                across = sides(sa, other)
+            pa = pa - da + square * (across - 2.0 * sa + ga - gsa)
+            if step < 3:
+                pb = pb - db + square * (sides(sb, given(B1 + step)) - 2.0 * sb + gb - gsb)
+                sa, sb = sa + pa, sb + pb
+        za = st[spot_of(0), :].reshape(shape) - COURANT * (ea - sa)
         ma = jnp.where(open_a, ma - COURANT * ga, 0.0)
-        z_west, _ = west(za, zc)
+        z_west = jnp.where(first_lane, given(ZF), turn(za, 1))
         share = (0.5 + 0.45 * jnp.tanh(za)).reshape(LC * ROWS, COLS)
         share_west = (0.5 + 0.45 * jnp.tanh(z_west)).reshape(LC * ROWS, COLS)
         for f, value in enumerate((za, ma, pa)):
-            spot = pl.ds(pl.multiple_of(f * FIELD + ch * LC * ROWS, ROWS), LC * ROWS)
-            st[spot, :] = value.reshape(LC * ROWS, COLS)
-        out[pl.ds(pl.multiple_of(2 * FIELD + ch * LC * ROWS, ROWS), LC * ROWS), :] = pa.reshape(LC * ROWS, COLS)
+            st[spot_of(f), :] = value.reshape(LC * ROWS, COLS)
+        out[spot_of(2), :] = pa.reshape(LC * ROWS, COLS)
         for f in range(4):
-            spot = pl.ds(pl.multiple_of(f * FIELD + ch * LC * ROWS, ROWS), LC * ROWS)
-            fr[spot, :] = share
-            fw[spot, :] = share_west
+            fr[spot_of(f), :] = share
+            fw[spot_of(f), :] = share_west
         return carry
 
     lax.fori_loop(0, NCH, acoustic, 0)
@@ -412,7 +464,8 @@
             q = st[pl.ds(3 * FIELD + j, 4 * LEV, stride=ROWS), :] + STEP * t[2 * LEV : 6 * LEV]
             qb[0, j] = q.astype(BF16)
             fl[pl.ds(j, 8, stride=ROWS), :] = t[6 * LEV :]
-        first_hops(n, lambda copy: copy.start())
+        for r in range(CH):
+            first_hops(n * CH + r, lambda copy: copy.start())
         return carry
 
     lax.fori_loop(0, NB, network, 0)
@@ -437,11 +490,14 @@
 
     forward(OZ)
 
-    def tracer_block(n, carry):
+    def tracer_row(n, carry):
         forward(n)
-        complete(n)
-        for r in range(CH):
-            advect(n * CH + r, qb, 4 * LEV, 3)
+
+        @pl.when(n > 0)
+        def _():
+            complete(n - 1)
+            advect(n - 1, qb, 4 * LEV, 3)
+
         return carry
 
     complete(OZ)
@@ -451,20 +507,11 @@
         return carry
 
     lax.fori_loop(0, ROWS, ozone_row, 0)
-    lax.fori_loop(0, NB, tracer_block, 0)
-
-    @pl.when(lat > 0)
-    def _():
-        edge_copy(2).wait_send()
-        edge_copy(3).wait_send()
-
-    @pl.when(lat < N_LAT - 1)
-    def _():
-        edge_copy(4).wait_send()
-        edge_copy(5).wait_send()
-
-    edge_copy(0).wait_send()
-    edge_copy(1).wait_send()
+    lax.fori_loop(0, ROWS, tracer_row, 0)
+    complete(ROWS - 1)
+    advect(ROWS - 1, qb, 4 * LEV, 3)
+
+    all_edges(lambda copy: copy.wait_send())
     for ch in range(NCH):
 
         @pl.when(lat > 0)
@@ -481,7 +528,7 @@
         drain(n)
         return carry
 
-    lax.fori_loop(0, NB, drain_block, 0)
+    lax.fori_loop(0, ROWS, drain_block, 0)
 
 
 def place(state, flux, state_out, flux_out, sem):
@@ -523,21 +570,24 @@
             pltpu.VMEM((4 * FIELD, COLS), F32),
             pltpu.VMEM((4 * FIELD, COLS), F32),
             pltpu.VMEM((8 * ROWS, COLS), F32),
-            pltpu.VMEM((2, NCH, 3 * HC * ROWS, COLS), BF16),
-            pltpu.VMEM((2, NCH, 3 * HC * ROWS, COLS), BF16),
-            pltpu.VMEM((3 * GROUPS * ROWS, COLS), BF16),
-            pltpu.VMEM((6, 3 * GROUPS * ROWS, COLS), BF16),
-            pltpu.VMEM((3 * GROUPS * ROWS, COLS), F32),
-            pltpu.VMEM((3 * GROUPS * ROWS, COLS), F32),
+            pltpu.VMEM((FIELD, COLS), F32),
+            pltpu.VMEM((2, NCH, LC * ROWS, COLS), BF16),
+            pltpu.VMEM((2, NCH, LC * ROWS, COLS), BF16),
+            pltpu.VMEM((EROWS, COLS), F32),
+            pltpu.VMEM((EROWS, COLS), BF16),
+            pltpu.VMEM((2, EROWS // 2, COLS), BF16),
+            pltpu.VMEM((2, EROWS, COLS), BF16),
+            pltpu.VMEM((6, EROWS // 2, COLS), BF16),
+            pltpu.VMEM((10, GROUPS * ROWS, COLS), F32),
             pltpu.VMEM((4, ROWS, LEV, COLS), BF16),
             pltpu.VMEM((4, ROWS, 4 * LEV, COLS), BF16),
             dma((9,)),
             dma((2, NCH)),
             dma((2, NCH)),
-            dma((6,)),
-            dma((6,)),
-            dma((NB + 1, 4)),
-            dma((NB + 1, 4)),
+            dma((8,)),
+            dma((8,)),
+            dma((ROWS + 1, 4)),
+            dma((ROWS + 1, 4)),
         ],
         compiler_params=pltpu.CompilerParams(
             collective_id=0, has_side_effects=True, vmem_limit_bytes=56 * 1024 * 1024

time: 37.9 us -> 34.8 us (0.918)
  Pallas kernels: 37.2 us -> 33.9 us
    pallas_call x1, Pallas kernels: 35.9 us -> 32.6 us  [on_device(): pl.pallas_call(kernel, out_shape=(pltpu.VMEM((fields * FIELD, COLS), F32)...]
where the time goes in v2:
time: 34.8 us; the launch traced here: 34.5 us
  Pallas kernels  33.9 us (97%)
  between operations  0.64 us (2%)
    pallas_call x1, Pallas kernels, on_device(): pl.pallas_call(kernel, out_shape=(pltpu.VMEM((fields * FIELD, COLS), F32)...  32.6 us
    pallas_call x1, Pallas kernels, on_device(): pl.pallas_call(place, out_shape=(jax.ShapeDtypeStruct((fields * FIELD, CO...  1.31 us

profile of v2, /device:TPU:23, one launch (start us, length us, event | category | flops | bytes accessed | tf_op | source)
XLA Modules:
  0.0 34.5 jit_solution(6009232999511816662)
XLA Ops:
  0.6 32.6 %shard_map.104 = (f32[3840,128]{1,0:T(8,128)S(1)}, bf16[64,128]{1,0:T(8,128)(2,1)S(1)}) custom-call(f32[3840,128]{1,0:T(8,128)} %bitcast.6, bf16[608,128]{1,0:T(8,128)(2,1)} %bitcast.8, bf16[556,768]{1,0:T(8,128)(2,1)} %w1h.1, bf16[768,640]{1,0:T(8,128)(2,1)} %w2h.1, bf16[640,512]{1,0:T(8,128)(2,1)} %w3h.1, bf16[512,640]{1,0:T(8,128)(2,1)} %w4h.1, ...), custom_call_target="tpu_custom_call" | custom-call | tf_op jit(solution)/shard_map/pallas_call | solution.py:550
  33.2 1.3 %shard_map.105 = (f32[3840,128]{1,0:T(8,128)}, bf16[64,128]{1,0:T(8,128)(2,1)}) custom-call(f32[3840,128]{1,0:T(8,128)S(1)} %get-tuple-element.6.state, bf16[64,128]{1,0:T(8,128)(2,1)S(1)} %get-tuple-element.7.flux), custom_call_target="tpu_custom_call" | custom-call | tf_op jit(solution)/shard_map/pallas_call | solution.py:602

commit v3 on v2

--- a/solution.py
+++ b/solution.py
@@ -25,8 +25,9 @@
 GROUPS = LEV // PER
 EROWS = 3 * GROUPS * ROWS
 CH = 2
+LAG_B, LAG_C = 1, 2
 NB = ROWS // CH
-OZ = ROWS
+OZ = NB
 
 AROUND = ((0, -1), (0, 1), (-1, 0), (1, 0), (-1, -1), (-1, 1), (1, -1), (1, 1))
 A1, B1, ZA, ZB, ZF = 0, 4, 7, 8, 9
@@ -76,7 +77,7 @@
     def greet(dlat, dlon):
         pl.semaphore_signal(barrier, inc=1, device_id=at(dlat, dlon), device_id_type=MESH)
 
-    for dlon in (-3, -2, -1, 1, 2, 3):
+    for dlon in (-4, -3, -2, -1, 1, 2, 3, 4):
         greet(0, dlon)
 
     @pl.when(lat > 0)
@@ -125,7 +126,7 @@
     hsend[0] = jnp.where(half, low, pltpu.roll(high, 4, 1)).reshape(EROWS // 2, COLS).astype(BF16)
     hsend[1] = jnp.where(half, pltpu.roll(low, 4, 1), high).reshape(EROWS // 2, COLS).astype(BF16)
 
-    neighbours = 6 + 3 * ((lat + N_LAT - 1) // N_LAT) + 3 * ((2 * N_LAT - 2 - lat) // N_LAT)
+    neighbours = 8 + 3 * ((lat + N_LAT - 1) // N_LAT) + 3 * ((2 * N_LAT - 2 - lat) // N_LAT)
     pl.semaphore_wait(barrier, neighbours)
 
     def row_copy(side, ch):
@@ -190,7 +191,7 @@
     def block(n, slot):
         if isinstance(n, int) and n == OZ:
             return oz.at[slot]
-        return qb.at[slot, n]
+        return qb.at[slot, pl.ds(n * CH, CH)]
 
     def send(n, flow, source, slot, dlon):
         return pltpu.make_async_remote_copy(
@@ -199,63 +200,75 @@
             device_id=at(0, dlon), device_id_type=MESH,
         )
 
+    def flow(name, n):
+        if name == "y" or name == "d":
+            return send(n, 0 if name == "d" else 1, 0, 2, 2)
+        if name == "z":
+            return send(n, 0, 0, 3, 3)
+        if name == "x":
+            return send(n, 0, 0, 4, 4)
+        if name == "s":
+            return send(n, 1, 4, 3, -1)
+        if name == "p":
+            return send(n, 2, 0, 1, 1)
+        if name == "r":
+            return send(n, 3, 4, 2, -2)
+        if name == "f":
+            return send(n, 4, 2, 3, 1)
+        return send(n, 4, 2, 1, -1)
+
+    sources = {
+        "y": quarter < 2, "d": quarter == 2, "z": quarter == 1, "x": quarter == 3, "p": core == 0,
+        "r": quarter == 3, "s": quarter == 3, "f": core == 0, "g": quarter == 3, "h": quarter == 1,
+    }
+    drains = {
+        "y": quarter >= 2, "d": quarter == 0, "z": quarter == 0, "x": quarter == 3, "p": core == 1,
+        "r": quarter == 1, "s": quarter == 2, "f": core == 1, "g": quarter == 2, "h": quarter == 0,
+    }
+
+    def do(name, n, act):
+        @pl.when(sources[name])
+        def _():
+            act(flow(name, n))
+
+    def got(name, n):
+        @pl.when(drains[name])
+        def _():
+            flow(name, n).wait_recv()
+
     def first_hops(n, act):
-        @pl.when(core == 0)
-        def _():
-            act(send(n, 0, 0, 2, 2))
-            act(send(n, 1, 0, 1, 1))
-
-        @pl.when(core == 1)
-        def _():
-            act(send(n, 0, 0, 3, 3))
-
-        @pl.when(quarter == 1)
-        def _():
-            act(send(n, 1, 0, 2, 2))
-
-    def arrived(n, slot):
-        send(n, 0, 0, slot, 1).wait_recv()
+        for name in "xdyzp":
+            do(name, n, act)
+
+    def begin(copy):
+        copy.start()
+
+    def relay(n):
+        got("x", n)
+        do("r", n, begin)
+        do("s", n, begin)
 
     def forward(n):
-        @pl.when(core == 0)
-        def _():
-            arrived(n, 3)
-
-        @pl.when(quarter == 2)
-        def _():
-            send(n, 2, 3, 2, -1).start()
-
-        arrived(n, 2)
-
-        @pl.when(core == 0)
-        def _():
-            send(n, 3, 2, 3, 1).start()
-
-        @pl.when(core == 1)
-        def _():
-            send(n, 3, 2, 1, -1).start()
+        got("d", n)
+        got("y", n)
+        do("f", n, begin)
+        do("g", n, begin)
+
+    def forward_relayed(n):
+        got("r", n)
+        do("h", n, begin)
 
     def complete(n):
-        arrived(n, 1)
-
-        @pl.when(core == 1)
-        def _():
-            arrived(n, 3)
+        got("z", n)
+        got("s", n)
+        got("p", n)
+        got("g", n)
+        got("h", n)
+        got("f", n)
 
     def drain(n):
-        first_hops(n, lambda copy: copy.wait_send())
-
-        @pl.when(quarter == 2)
-        def _():
-            send(n, 2, 3, 2, -1).wait_send()
-
-        @pl.when(core == 0)
-        def _():
-            send(n, 3, 2, 3, 1).wait_send()
-
-        @pl.when(core == 1)
-        def _():
-            send(n, 3, 2, 1, -1).wait_send()
+        for name in "ydzxprsfgh":
+            do(name, n, lambda copy: copy.wait_send())
 
     loads[1].wait()
     for j in range(ROWS):
@@ -443,6 +456,8 @@
 
     lax.fori_loop(0, NCH, acoustic, 0)
 
+    relay(OZ)
+    forward(OZ)
     for load in loads[6:]:
         load.wait()
 
@@ -460,15 +475,24 @@
         for r in range(CH):
             j = n * CH + r
             t = jnp.where(jnp.broadcast_to(mask[pl.ds(j, 1), :], (NOUT, COLS)) > 0.5, y[:, r * COLS : (r + 1) * COLS], 0.0)
-            out[pl.ds(j, 2 * LEV, stride=ROWS), :] = st[pl.ds(j, 2 * LEV, stride=ROWS), :] + STEP * t[0 : 2 * LEV]
             q = st[pl.ds(3 * FIELD + j, 4 * LEV, stride=ROWS), :] + STEP * t[2 * LEV : 6 * LEV]
             qb[0, j] = q.astype(BF16)
+            out[pl.ds(j, 2 * LEV, stride=ROWS), :] = st[pl.ds(j, 2 * LEV, stride=ROWS), :] + STEP * t[0 : 2 * LEV]
             fl[pl.ds(j, 8, stride=ROWS), :] = t[6 * LEV :]
-        for r in range(CH):
-            first_hops(n * CH + r, lambda copy: copy.start())
+        first_hops(n, begin)
         return carry
 
-    lax.fori_loop(0, NB, network, 0)
+    lax.fori_loop(0, ROWS // CH, network, 0)
+    forward_relayed(OZ)
+
+    @pl.when(quarter == 3)
+    def _():
+        def relay_row(n, carry):
+            relay(n)
+            return carry
+
+        lax.fori_loop(0, NB, relay_row, 0)
+
     flux[...] = fl[...].astype(BF16)
 
     def advect(j, ref, count, base):
@@ -488,18 +512,6 @@
         value = (1.0 - fr[spot, :]) * near + fw[spot, :] * far
         out[pl.ds(base * FIELD + j, count, stride=ROWS), :] = value
 
-    forward(OZ)
-
-    def tracer_row(n, carry):
-        forward(n)
-
-        @pl.when(n > 0)
-        def _():
-            complete(n - 1)
-            advect(n - 1, qb, 4 * LEV, 3)
-
-        return carry
-
     complete(OZ)
 
     def ozone_row(j, carry):
@@ -507,9 +519,25 @@
         return carry
 
     lax.fori_loop(0, ROWS, ozone_row, 0)
-    lax.fori_loop(0, ROWS, tracer_row, 0)
-    complete(ROWS - 1)
-    advect(ROWS - 1, qb, 4 * LEV, 3)
+
+    def step(k, carry):
+        @pl.when(k < NB)
+        def _():
+            forward(k)
+
+        @pl.when(jnp.logical_and(k >= LAG_B, k < NB + LAG_B))
+        def _():
+            forward_relayed(k - LAG_B)
+
+        @pl.when(k >= LAG_C)
+        def _():
+            complete(k - LAG_C)
+            for r in range(CH):
+                advect((k - LAG_C) * CH + r, qb, 4 * LEV, 3)
+
+        return carry
+
+    lax.fori_loop(0, NB + LAG_C, step, 0)
 
     all_edges(lambda copy: copy.wait_send())
     for ch in range(NCH):
@@ -528,7 +556,7 @@
         drain(n)
         return carry
 
-    lax.fori_loop(0, ROWS, drain_block, 0)
+    lax.fori_loop(0, NB, drain_block, 0)
 
 
 def place(state, flux, state_out, flux_out, sem):
@@ -579,15 +607,15 @@
             pltpu.VMEM((2, EROWS, COLS), BF16),
             pltpu.VMEM((6, EROWS // 2, COLS), BF16),
             pltpu.VMEM((10, GROUPS * ROWS, COLS), F32),
-            pltpu.VMEM((4, ROWS, LEV, COLS), BF16),
-            pltpu.VMEM((4, ROWS, 4 * LEV, COLS), BF16),
+            pltpu.VMEM((5, ROWS, LEV, COLS), BF16),
+            pltpu.VMEM((5, ROWS, 4 * LEV, COLS), BF16),
             dma((9,)),
             dma((2, NCH)),
             dma((2, NCH)),
             dma((8,)),
             dma((8,)),
-            dma((ROWS + 1, 4)),
-            dma((ROWS + 1, 4)),
+            dma((NB + 1, 5)),
+            dma((NB + 1, 5)),
         ],
         compiler_params=pltpu.CompilerParams(
             collective_id=0, has_side_effects=True, vmem_limit_bytes=56 * 1024 * 1024

time: 34.8 us -> 34.1 us (0.980)
  the two profiles are of different devices: /device:TPU:23 before, /device:TPU:1 now
where the time goes in v3:
time: 34.1 us; the launch traced here: 33.9 us
  Pallas kernels  33.3 us (98%)
  between operations  0.64 us (2%)
    pallas_call x1, Pallas kernels, on_device(): pl.pallas_call(kernel, out_shape=(pltpu.VMEM((fields * FIELD, COLS), F32)...  32 us
    pallas_call x1, Pallas kernels, on_device(): pl.pallas_call(place, out_shape=(jax.ShapeDtypeStruct((fields * FIELD, CO...  1.31 us

profile of v3, /device:TPU:1, one launch (start us, length us, event | category | flops | bytes accessed | tf_op | source)
XLA Modules:
  0.0 33.9 jit_solution(3720398089973594679)
XLA Ops:
  0.6 32.0 %shard_map.104 = (f32[3840,128]{1,0:T(8,128)S(1)}, bf16[64,128]{1,0:T(8,128)(2,1)S(1)}) custom-call(f32[3840,128]{1,0:T(8,128)} %bitcast.6, bf16[608,128]{1,0:T(8,128)(2,1)} %bitcast.8, bf16[556,768]{1,0:T(8,128)(2,1)} %w1h.1, bf16[768,640]{1,0:T(8,128)(2,1)} %w2h.1, bf16[640,512]{1,0:T(8,128)(2,1)} %w3h.1, bf16[512,640]{1,0:T(8,128)(2,1)} %w4h.1, ...), custom_call_target="tpu_custom_call" | custom-call | tf_op jit(solution)/shard_map/pallas_call | solution.py:578
  32.6 1.3 %shard_map.105 = (f32[3840,128]{1,0:T(8,128)}, bf16[64,128]{1,0:T(8,128)(2,1)}) custom-call(f32[3840,128]{1,0:T(8,128)S(1)} %get-tuple-element.6.state, bf16[64,128]{1,0:T(8,128)(2,1)S(1)} %get-tuple-element.7.flux), custom_call_target="tpu_custom_call" | custom-call | tf_op jit(solution)/shard_map/pallas_call | solution.py:630

commit v4 on v3

--- a/solution.py
+++ b/solution.py
@@ -209,6 +209,8 @@
             return send(n, 0, 0, 4, 4)
         if name == "s":
             return send(n, 1, 4, 3, -1)
+        if name == "e":
+            return send(n, 3, 0, 2, 2)
         if name == "p":
             return send(n, 2, 0, 1, 1)
         if name == "r":
@@ -219,7 +221,7 @@
 
     sources = {
         "y": quarter < 2, "d": quarter == 2, "z": quarter == 1, "x": quarter == 3, "p": core == 0,
-        "r": quarter == 3, "s": quarter == 3, "f": core == 0, "g": quarter == 3, "h": quarter == 1,
+        "r": quarter == 3, "e": quarter == 3, "s": quarter == 3, "f": core == 0, "g": quarter == 3, "h": quarter == 1,
     }
     drains = {
         "y": quarter >= 2, "d": quarter == 0, "z": quarter == 0, "x": quarter == 3, "p": core == 1,
@@ -243,9 +245,25 @@
     def begin(copy):
         copy.start()
 
+    def relayed(n, act):
+        if isinstance(n, int):
+            do("r", n, act)
+        else:
+
+            @pl.when(n > 0)
+            def _():
+                do("r", n, act)
+
+    def straight(n, act):
+        if not isinstance(n, int):
+
+            @pl.when(n == 0)
+            def _():
+                do("e", n, act)
+
     def relay(n):
         got("x", n)
-        do("r", n, begin)
+        relayed(n, begin)
         do("s", n, begin)
 
     def forward(n):
@@ -267,8 +285,13 @@
         got("f", n)
 
     def drain(n):
-        for name in "ydzxprsfgh":
-            do(name, n, lambda copy: copy.wait_send())
+        def sent(copy):
+            copy.wait_send()
+
+        for name in "ydzxpsfgh":
+            do(name, n, sent)
+        relayed(n, sent)
+        straight(n, sent)
 
     loads[1].wait()
     for j in range(ROWS):
@@ -480,6 +503,7 @@
             out[pl.ds(j, 2 * LEV, stride=ROWS), :] = st[pl.ds(j, 2 * LEV, stride=ROWS), :] + STEP * t[0 : 2 * LEV]
             fl[pl.ds(j, 8, stride=ROWS), :] = t[6 * LEV :]
         first_hops(n, begin)
+        straight(n, begin)
         return carry
 
     lax.fori_loop(0, ROWS // CH, network, 0)

time: 34.1 us -> 33.3 us (0.977)
  the two profiles are of different devices: /device:TPU:1 before, /device:TPU:6 now
where the time goes in v4:
time: 33.3 us; the launch traced here: 33.1 us
  Pallas kernels  32.5 us (98%)
  between operations  0.64 us (2%)
    pallas_call x1, Pallas kernels, on_device(): pl.pallas_call(kernel, out_shape=(pltpu.VMEM((fields * FIELD, COLS), F32)...  31.2 us
    pallas_call x1, Pallas kernels, on_device(): pl.pallas_call(place, out_shape=(jax.ShapeDtypeStruct((fields * FIELD, CO...  1.31 us

profile of v4, /device:TPU:6, one launch (start us, length us, event | category | flops | bytes accessed | tf_op | source)
XLA Modules:
  0.0 33.1 jit_solution(13127000923559552050)
XLA Ops:
  0.6 31.2 %shard_map.104 = (f32[3840,128]{1,0:T(8,128)S(1)}, bf16[64,128]{1,0:T(8,128)(2,1)S(1)}) custom-call(f32[3840,128]{1,0:T(8,128)} %bitcast.6, bf16[608,128]{1,0:T(8,128)(2,1)} %bitcast.8, bf16[556,768]{1,0:T(8,128)(2,1)} %w1h.1, bf16[768,640]{1,0:T(8,128)(2,1)} %w2h.1, bf16[640,512]{1,0:T(8,128)(2,1)} %w3h.1, bf16[512,640]{1,0:T(8,128)(2,1)} %w4h.1, ...), custom_call_target="tpu_custom_call" | custom-call | tf_op jit(solution)/shard_map/pallas_call | solution.py:602
  31.8 1.3 %shard_map.105 = (f32[3840,128]{1,0:T(8,128)}, bf16[64,128]{1,0:T(8,128)(2,1)}) custom-call(f32[3840,128]{1,0:T(8,128)S(1)} %get-tuple-element.6.state, bf16[64,128]{1,0:T(8,128)(2,1)S(1)} %get-tuple-element.7.flux), custom_call_target="tpu_custom_call" | custom-call | tf_op jit(solution)/shard_map/pallas_call | solution.py:654

commit v5 on v4

--- a/solution.py
+++ b/solution.py
@@ -15,6 +15,7 @@
 COURANT = 0.6
 STEP = 0.5
 SLOPE = 0.15
+SPARE = 64
 DYN = 192
 NIN, NOUT = 556, 368
 H1, H2, H3, H4 = 768, 640, 512, 640
@@ -298,7 +299,7 @@
         oz[0, j] = st[pl.ds(7 * FIELD + j, LEV, stride=ROWS), :].astype(BF16)
     first_hops(OZ, lambda copy: copy.start())
     loads[2].wait()
-    sf[...] = sfb[...].astype(F32)
+    sf[0 : 76 * ROWS] = sfb[...].astype(F32)
     loads[3].wait()
     listed = lit[...]
     row_id = lax.broadcasted_iota(jnp.int32, (ROWS, COLS), 0)
@@ -308,7 +309,7 @@
         entry = listed[r : r + 1]
         in_row.append(jnp.where(jnp.broadcast_to(entry >> 7, (ROWS, COLS)) == row_id, 1.0, 0.0))
         in_col.append(jnp.where(jnp.broadcast_to(entry & 127, (COLS, COLS)) == col_id, 1.0, 0.0))
-    mask[...] = nt(jnp.concatenate(in_row, 1).astype(BF16), jnp.concatenate(in_col, 1).astype(BF16))
+    mask[0:ROWS] = nt(jnp.concatenate(in_row, 1).astype(BF16), jnp.concatenate(in_col, 1).astype(BF16))
     loads[4].wait()
     eye_c = eye(COLS)
 
@@ -602,15 +603,15 @@
     new_state, surface_flux = pl.pallas_call(
         kernel,
         out_shape=(
-            pltpu.VMEM((fields * FIELD, COLS), F32),
+            pltpu.VMEM((fields * FIELD + SPARE, COLS), F32),
             pltpu.VMEM((8 * ROWS, COLS), BF16),
         ),
         in_specs=[any_spec] * 8 + [pl.BlockSpec(memory_space=pltpu.SMEM)],
         out_specs=(vmem_spec, vmem_spec),
         scratch_shapes=[
-            pltpu.VMEM((fields * FIELD, COLS), F32),
+            pltpu.VMEM((fields * FIELD + SPARE, COLS), F32),
             pltpu.VMEM((76 * ROWS, COLS), BF16),
-            pltpu.VMEM((76 * ROWS, COLS), F32),
+            pltpu.VMEM((76 * ROWS + SPARE, COLS), F32),
             pltpu.VMEM((NIN, H1), BF16),
             pltpu.VMEM((H1, H2), BF16),
             pltpu.VMEM((H2, H3), BF16),
@@ -618,7 +619,7 @@
             pltpu.VMEM((NOUT, H4), BF16),
             pltpu.VMEM((ROWS, COLS), jnp.int32),
             pltpu.VMEM((ROWS * COLS, H1), F32),
-            pltpu.VMEM((ROWS, COLS), F32),
+            pltpu.VMEM((2 * ROWS, COLS), F32),
             pltpu.VMEM((4 * FIELD, COLS), F32),
             pltpu.VMEM((4 * FIELD, COLS), F32),
             pltpu.VMEM((8 * ROWS, COLS), F32),

time: 33.3 us -> 33.2 us (level)
  no operation moved by 1% of the time
where the time goes in v5:
time: 33.2 us; the launch traced here: 33.1 us
  Pallas kernels  32.5 us (98%)
  between operations  0.64 us (2%)
    pallas_call x1, Pallas kernels, on_device(): pl.pallas_call(kernel, out_shape=(pltpu.VMEM((fields * FIELD + SPARE, COL...  31.2 us
    pallas_call x1, Pallas kernels, on_device(): pl.pallas_call(place, out_shape=(jax.ShapeDtypeStruct((fields * FIELD, CO...  1.31 us

profile of v5, /device:TPU:6, one launch (start us, length us, event | category | flops | bytes accessed | tf_op | source)
XLA Modules:
  0.0 33.1 jit_solution(18333542391206223320)
XLA Ops:
  0.6 31.2 %shard_map.104 = (f32[3904,128]{1,0:T(8,128)S(1)}, bf16[64,128]{1,0:T(8,128)(2,1)S(1)}) custom-call(f32[3840,128]{1,0:T(8,128)} %bitcast.6, bf16[608,128]{1,0:T(8,128)(2,1)} %bitcast.8, bf16[556,768]{1,0:T(8,128)(2,1)} %w1h.1, bf16[768,640]{1,0:T(8,128)(2,1)} %w2h.1, bf16[640,512]{1,0:T(8,128)(2,1)} %w3h.1, bf16[512,640]{1,0:T(8,128)(2,1)} %w4h.1, ...), custom_call_target="tpu_custom_call" | custom-call | tf_op jit(solution)/shard_map/pallas_call | solution.py:603
  31.8 1.3 %shard_map.105 = (f32[3840,128]{1,0:T(8,128)}, bf16[64,128]{1,0:T(8,128)(2,1)}) custom-call(f32[3904,128]{1,0:T(8,128)S(1)} %get-tuple-element.6.state, bf16[64,128]{1,0:T(8,128)(2,1)S(1)} %get-tuple-element.7.flux), custom_call_target="tpu_custom_call" | custom-call | tf_op jit(solution)/shard_map/pallas_call | solution.py:655
